TPU v7x, 32 devices: a whole 2x2x4 slice. The times are simulated.
32 devices in a mesh: pair: 8 (over z, y), aux: 4 (over x, core).
Axes of the slice: x: 2, y: 2, z: 4, core: 2. Of those that a mesh axis runs over, the one named last changes fastest.
Arguments:
- ints_ac: bfloat16 [192, 512, 4096], P(None, ('pair', 'aux')), may hold values from -0.375 to 0.375
- slot_pair: int32 [192], replicated, may hold values from 0 to 191, each once
- amplitudes: bfloat16 [192, 2, 4096], P(('pair', 'aux')), may hold values from -6 to 6
- ranks: int32 [192], P(('pair', 'aux')), may hold values from 16 to 64
- pair_occ: int32 [192, 2], P(('pair', 'aux')), may hold values from 0 to 47
- pno_energy: float32 [192, 64], P(('pair', 'aux')), may hold values from 0.2 to 3
- occ_energy: float32 [48], replicated, may hold values from -2 to -0.3
Outputs:
- ext_residual: float32 [192, 2, 4096], P(('pair', 'aux'))
- new_amplitudes: bfloat16 [192, 2, 4096], P(('pair', 'aux'))
Inputs may be any that keep to these rules, and one draw needn't show every extreme that they name: `slot_pair`: a permutation of the pairs. Entries a >= ranks[s] of a slot's blocks are padding.
All inputs are finite; a program needn't handle non-finite values.
Results may differ from a plain program's by a relative error of at most 0.0039.
Values may be sent and summed in bfloat16 or wider, within the bound.
A program may use at most 128 MiB of HBM per device.

v0:
```python
import jax
import jax.numpy as jnp
from jax import lax
from jax.sharding import PartitionSpec as P


def contract(blocks_in, amps_in, mask_in):
    width = mask_in.shape[0]
    count = blocks_in.shape[0]
    square = (mask_in[:, None] * mask_in[None, :]).reshape(width * width)
    masked_b = (blocks_in * square).reshape(count, width, width)
    masked_t = (amps_in * square).reshape(2, width, width)
    first = jnp.einsum(
        "pac,cd->pad", masked_b, masked_t[0], preferred_element_type=jnp.float32
    ).astype(jnp.bfloat16)
    second = jnp.einsum(
        "pac,cd->pad", masked_b, masked_t[1], preferred_element_type=jnp.float32
    ).astype(jnp.bfloat16)
    result = jnp.stack(
        [
            jnp.einsum("pad,pbd->ab", first, masked_b, preferred_element_type=jnp.float32),
            jnp.einsum("pad,pbd->ab", second, masked_b, preferred_element_type=jnp.float32),
        ]
    )
    return result.reshape(2, width * width)


def body(ints_ac, slot_pair, amplitudes, ranks, pair_occ, pno_energy, occ_energy):
    width = pno_energy.shape[1]
    local = amplitudes.shape[0]
    positions = jnp.arange(width, dtype=jnp.int32)
    masks = (positions[None, :] < ranks[:, None]).astype(jnp.float32)
    mask_half = masks.astype(jnp.bfloat16)
    every_amps, every_mask = (
        lax.all_gather(amplitudes, ("pair", "aux"), axis=0, tiled=True),
        lax.all_gather(mask_half, ("pair", "aux"), axis=0, tiled=True),
    )
    aux_local = ints_ac.shape[1]
    count = local * lax.axis_size(("pair", "aux"))
    batch = 1
    for guess in range(1, count + 1):
        if count % guess == 0 and guess * aux_local <= 256:
            batch = guess
    turns = count // batch

    def per_block(items):
        picked = jnp.take(ints_ac, items[0], axis=0)
        return jax.vmap(contract)(picked, items[1], items[2])

    out = lax.map(
        per_block,
        (
            slot_pair.reshape(turns, batch),
            every_amps.reshape(turns, batch, 2, width * width),
            every_mask.reshape(turns, batch, width),
        ),
    )
    residual = lax.psum_scatter(
        out.reshape(count, 2, width * width), ("pair", "aux"), scatter_dimension=0, tiled=True
    )
    onehot = (
        pair_occ[:, :, None] == jnp.arange(occ_energy.shape[0], dtype=jnp.int32)[None, None, :]
    ).astype(jnp.float32)
    occ_pair = jnp.einsum("jko,o->jk", onehot, occ_energy, precision=lax.Precision.HIGHEST)
    denom = (
        pno_energy[:, :, None]
        + pno_energy[:, None, :]
        - (occ_pair[:, 0] + occ_pair[:, 1])[:, None, None]
    )
    square = masks[:, :, None] * masks[:, None, :]
    masked_t = amplitudes.astype(jnp.float32).reshape(local, 2, width, width) * square[:, None]
    updated = (masked_t - residual.reshape(local, 2, width, width) / denom[:, None]) * square[
        :, None
    ]
    return (residual, updated.reshape(local, 2, width * width).astype(jnp.bfloat16))


def solution(mesh):
    placed = (
        P(None, ("pair", "aux"), None),
        P(),
        P(("pair", "aux"), None, None),
        P(("pair", "aux")),
        P(("pair", "aux"), None),
        P(("pair", "aux"), None),
        P(),
    )
    return jax.shard_map(
        body,
        mesh=mesh,
        in_specs=placed,
        out_specs=(P(("pair", "aux"), None, None), P(("pair", "aux"), None, None)),
        check_vma=False,
    )
```

profile of v0, /device:TPU:0, one launch (start us, length us, event | category | flops | bytes accessed | tf_op | source)
XLA Modules:
  0.0 600.9 jit_solution(4224171123640283326)
XLA Ops:
  9.5 43.6 %all-gather = bf16[32,6,64]{2,1,0:T(8,128)(2,1)S(1)} all-gather(bf16[1,6,64]{2,1,0:T(8,128)(2,1)S(1)} %get-tuple-element.55), channel_id=1, replica_groups=mesh['pair'=8,'aux'=4] {'pair','aux'}, dimensions={0}, use_global_device_ids=true | all-gather | bytes 25344 | tf_op jit(solution)/shard_map/all_gather | solution.py:36
  53.1 19.6 %all-gather.3.cloned.1.call-done = bf16[192,2,4096]{2,1,0:T(2,128)(2,1)} async-done(((bf16[6,2,4096]{2,1,0:T(2,128)(2,1)}), bf16[192,2,4096]{2,1,0:T(2,128)(2,1)}) %all-gather.3.cloned.1.call-update) | async-done | bytes 3145744 | tf_op jit(solution)/shard_map/all_gather | solution.py:35
  72.7 364.8 %while.10 = (s32[]{:T(128)}, f32[12,16,2,4096]{3,2,1,0:T(2,128)}, s32[12,16]{1,0:T(8,128)S(1)}, bf16[192,16,4096]{2,1,0:T(8,128)(2,1)}, bf16[12,16,64]{2,1,0:T(8...) while((s32[]{:T(128)}, f32[12,16,2,4096]{3,2,1,0:T(2,128)}, s32[12,16]{1,0:T(8,128)S(1)}, ...), condition=%wide.region_1.2_spmd, body=%wide.region_0.1_spmd.sunk | while | flops 547685504 | bytes 32780728 | solution.py:50
  72.7 8.8 %gather_fusion = bf16[16,16,4096]{2,1,0:T(8,128)(2,1)S(1)} fusion(bf16[192,16,4096]{2,1,0:T(8,128)(2,1)} %get-tuple-element.111, s32[1024]{0:T(1024)S(1)} %pad_clamp_fusion.2), kind=kCustom, calls=%fused_computation.clone.1 | custom fusion | bytes 4194368 | tf_op jit(solution)/shard_map/while/body/eval_jaxpr/jit(_take)/gather | solution.py:47
  95.3 6.0 %fusion.32 = f32[1,16,64,64]{3,2,1,0:T(8,128)S(1)} fusion(bf16[16,16,64,64]{3,2,1,0:T(8,128)(2,1)} %gather.11, pred[16]{0:T(512)(128)(4,1)S(1)} %compare_and_fusion.2, bf16[16,64,64]{2,1,0:T(8,128)(2,1)S(1)} %broadcast_multiply_fusion.5, bf16[16,2,64,64]{3,2,0,1:T(8,128)(2,1)S(1)} %broadcast_multiply_fusion.6), kind=kOutput, calls=%fused_computation.8.clone.1 | convolution fusion | flops 273678336 | bytes 9438208 | tf_op jit(solution)/shard_map/while/body/eval_jaxpr/vmap(pad,pbd->ab)/dot_general | solution.py:21
  103.1 8.8 %gather_fusion = bf16[16,16,4096]{2,1,0:T(8,128)(2,1)S(1)} fusion(bf16[192,16,4096]{2,1,0:T(8,128)(2,1)} %get-tuple-element.111, s32[1024]{0:T(1024)S(1)} %pad_clamp_fusion.2), kind=kCustom, calls=%fused_computation.clone.1 | custom fusion | bytes 4194368 | tf_op jit(solution)/shard_map/while/body/eval_jaxpr/jit(_take)/gather | solution.py:47
  125.7 6.0 %fusion.32 = f32[1,16,64,64]{3,2,1,0:T(8,128)S(1)} fusion(bf16[16,16,64,64]{3,2,1,0:T(8,128)(2,1)} %gather.11, pred[16]{0:T(512)(128)(4,1)S(1)} %compare_and_fusion.2, bf16[16,64,64]{2,1,0:T(8,128)(2,1)S(1)} %broadcast_multiply_fusion.5, bf16[16,2,64,64]{3,2,0,1:T(8,128)(2,1)S(1)} %broadcast_multiply_fusion.6), kind=kOutput, calls=%fused_computation.8.clone.1 | convolution fusion | flops 273678336 | bytes 9438208 | tf_op jit(solution)/shard_map/while/body/eval_jaxpr/vmap(pad,pbd->ab)/dot_general | solution.py:21
  133.5 8.8 %gather_fusion = bf16[16,16,4096]{2,1,0:T(8,128)(2,1)S(1)} fusion(bf16[192,16,4096]{2,1,0:T(8,128)(2,1)} %get-tuple-element.111, s32[1024]{0:T(1024)S(1)} %pad_clamp_fusion.2), kind=kCustom, calls=%fused_computation.clone.1 | custom fusion | bytes 4194368 | tf_op jit(solution)/shard_map/while/body/eval_jaxpr/jit(_take)/gather | solution.py:47
  156.1 6.0 %fusion.32 = f32[1,16,64,64]{3,2,1,0:T(8,128)S(1)} fusion(bf16[16,16,64,64]{3,2,1,0:T(8,128)(2,1)} %gather.11, pred[16]{0:T(512)(128)(4,1)S(1)} %compare_and_fusion.2, bf16[16,64,64]{2,1,0:T(8,128)(2,1)S(1)} %broadcast_multiply_fusion.5, bf16[16,2,64,64]{3,2,0,1:T(8,128)(2,1)S(1)} %broadcast_multiply_fusion.6), kind=kOutput, calls=%fused_computation.8.clone.1 | convolution fusion | flops 273678336 | bytes 9438208 | tf_op jit(solution)/shard_map/while/body/eval_jaxpr/vmap(pad,pbd->ab)/dot_general | solution.py:21
  163.9 8.8 %gather_fusion = bf16[16,16,4096]{2,1,0:T(8,128)(2,1)S(1)} fusion(bf16[192,16,4096]{2,1,0:T(8,128)(2,1)} %get-tuple-element.111, s32[1024]{0:T(1024)S(1)} %pad_clamp_fusion.2), kind=kCustom, calls=%fused_computation.clone.1 | custom fusion | bytes 4194368 | tf_op jit(solution)/shard_map/while/body/eval_jaxpr/jit(_take)/gather | solution.py:47
  186.5 6.0 %fusion.32 = f32[1,16,64,64]{3,2,1,0:T(8,128)S(1)} fusion(bf16[16,16,64,64]{3,2,1,0:T(8,128)(2,1)} %gather.11, pred[16]{0:T(512)(128)(4,1)S(1)} %compare_and_fusion.2, bf16[16,64,64]{2,1,0:T(8,128)(2,1)S(1)} %broadcast_multiply_fusion.5, bf16[16,2,64,64]{3,2,0,1:T(8,128)(2,1)S(1)} %broadcast_multiply_fusion.6), kind=kOutput, calls=%fused_computation.8.clone.1 | convolution fusion | flops 273678336 | bytes 9438208 | tf_op jit(solution)/shard_map/while/body/eval_jaxpr/vmap(pad,pbd->ab)/dot_general | solution.py:21
  194.3 8.8 %gather_fusion = bf16[16,16,4096]{2,1,0:T(8,128)(2,1)S(1)} fusion(bf16[192,16,4096]{2,1,0:T(8,128)(2,1)} %get-tuple-element.111, s32[1024]{0:T(1024)S(1)} %pad_clamp_fusion.2), kind=kCustom, calls=%fused_computation.clone.1 | custom fusion | bytes 4194368 | tf_op jit(solution)/shard_map/while/body/eval_jaxpr/jit(_take)/gather | solution.py:47
  224.7 8.8 %gather_fusion = bf16[16,16,4096]{2,1,0:T(8,128)(2,1)S(1)} fusion(bf16[192,16,4096]{2,1,0:T(8,128)(2,1)} %get-tuple-element.111, s32[1024]{0:T(1024)S(1)} %pad_clamp_fusion.2), kind=kCustom, calls=%fused_computation.clone.1 | custom fusion | bytes 4194368 | tf_op jit(solution)/shard_map/while/body/eval_jaxpr/jit(_take)/gather | solution.py:47
  247.3 6.0 %fusion.32 = f32[1,16,64,64]{3,2,1,0:T(8,128)S(1)} fusion(bf16[16,16,64,64]{3,2,1,0:T(8,128)(2,1)} %gather.11, pred[16]{0:T(512)(128)(4,1)S(1)} %compare_and_fusion.2, bf16[16,64,64]{2,1,0:T(8,128)(2,1)S(1)} %broadcast_multiply_fusion.5, bf16[16,2,64,64]{3,2,0,1:T(8,128)(2,1)S(1)} %broadcast_multiply_fusion.6), kind=kOutput, calls=%fused_computation.8.clone.1 | convolution fusion | flops 273678336 | bytes 9438208 | tf_op jit(solution)/shard_map/while/body/eval_jaxpr/vmap(pad,pbd->ab)/dot_general | solution.py:21
  255.1 8.8 %gather_fusion = bf16[16,16,4096]{2,1,0:T(8,128)(2,1)S(1)} fusion(bf16[192,16,4096]{2,1,0:T(8,128)(2,1)} %get-tuple-element.111, s32[1024]{0:T(1024)S(1)} %pad_clamp_fusion.2), kind=kCustom, calls=%fused_computation.clone.1 | custom fusion | bytes 4194368 | tf_op jit(solution)/shard_map/while/body/eval_jaxpr/jit(_take)/gather | solution.py:47
  277.7 6.0 %fusion.32 = f32[1,16,64,64]{3,2,1,0:T(8,128)S(1)} fusion(bf16[16,16,64,64]{3,2,1,0:T(8,128)(2,1)} %gather.11, pred[16]{0:T(512)(128)(4,1)S(1)} %compare_and_fusion.2, bf16[16,64,64]{2,1,0:T(8,128)(2,1)S(1)} %broadcast_multiply_fusion.5, bf16[16,2,64,64]{3,2,0,1:T(8,128)(2,1)S(1)} %broadcast_multiply_fusion.6), kind=kOutput, calls=%fused_computation.8.clone.1 | convolution fusion | flops 273678336 | bytes 9438208 | tf_op jit(solution)/shard_map/while/body/eval_jaxpr/vmap(pad,pbd->ab)/dot_general | solution.py:21
  285.5 8.8 %gather_fusion = bf16[16,16,4096]{2,1,0:T(8,128)(2,1)S(1)} fusion(bf16[192,16,4096]{2,1,0:T(8,128)(2,1)} %get-tuple-element.111, s32[1024]{0:T(1024)S(1)} %pad_clamp_fusion.2), kind=kCustom, calls=%fused_computation.clone.1 | custom fusion | bytes 4194368 | tf_op jit(solution)/shard_map/while/body/eval_jaxpr/jit(_take)/gather | solution.py:47
  315.9 8.8 %gather_fusion = bf16[16,16,4096]{2,1,0:T(8,128)(2,1)S(1)} fusion(bf16[192,16,4096]{2,1,0:T(8,128)(2,1)} %get-tuple-element.111, s32[1024]{0:T(1024)S(1)} %pad_clamp_fusion.2), kind=kCustom, calls=%fused_computation.clone.1 | custom fusion | bytes 4194368 | tf_op jit(solution)/shard_map/while/body/eval_jaxpr/jit(_take)/gather | solution.py:47
  346.3 8.8 %gather_fusion = bf16[16,16,4096]{2,1,0:T(8,128)(2,1)S(1)} fusion(bf16[192,16,4096]{2,1,0:T(8,128)(2,1)} %get-tuple-element.111, s32[1024]{0:T(1024)S(1)} %pad_clamp_fusion.2), kind=kCustom, calls=%fused_computation.clone.1 | custom fusion | bytes 4194368 | tf_op jit(solution)/shard_map/while/body/eval_jaxpr/jit(_take)/gather | solution.py:47
  368.9 6.0 %fusion.32 = f32[1,16,64,64]{3,2,1,0:T(8,128)S(1)} fusion(bf16[16,16,64,64]{3,2,1,0:T(8,128)(2,1)} %gather.11, pred[16]{0:T(512)(128)(4,1)S(1)} %compare_and_fusion.2, bf16[16,64,64]{2,1,0:T(8,128)(2,1)S(1)} %broadcast_multiply_fusion.5, bf16[16,2,64,64]{3,2,0,1:T(8,128)(2,1)S(1)} %broadcast_multiply_fusion.6), kind=kOutput, calls=%fused_computation.8.clone.1 | convolution fusion | flops 273678336 | bytes 9438208 | tf_op jit(solution)/shard_map/while/body/eval_jaxpr/vmap(pad,pbd->ab)/dot_general | solution.py:21
  376.6 8.8 %gather_fusion = bf16[16,16,4096]{2,1,0:T(8,128)(2,1)S(1)} fusion(bf16[192,16,4096]{2,1,0:T(8,128)(2,1)} %get-tuple-element.111, s32[1024]{0:T(1024)S(1)} %pad_clamp_fusion.2), kind=kCustom, calls=%fused_computation.clone.1 | custom fusion | bytes 4194368 | tf_op jit(solution)/shard_map/while/body/eval_jaxpr/jit(_take)/gather | solution.py:47
  407.1 8.8 %gather_fusion = bf16[16,16,4096]{2,1,0:T(8,128)(2,1)S(1)} fusion(bf16[192,16,4096]{2,1,0:T(8,128)(2,1)} %get-tuple-element.111, s32[1024]{0:T(1024)S(1)} %pad_clamp_fusion.2), kind=kCustom, calls=%fused_computation.clone.1 | custom fusion | bytes 4194368 | tf_op jit(solution)/shard_map/while/body/eval_jaxpr/jit(_take)/gather | solution.py:47
  429.7 6.0 %fusion.32 = f32[1,16,64,64]{3,2,1,0:T(8,128)S(1)} fusion(bf16[16,16,64,64]{3,2,1,0:T(8,128)(2,1)} %gather.11, pred[16]{0:T(512)(128)(4,1)S(1)} %compare_and_fusion.2, bf16[16,64,64]{2,1,0:T(8,128)(2,1)S(1)} %broadcast_multiply_fusion.5, bf16[16,2,64,64]{3,2,0,1:T(8,128)(2,1)S(1)} %broadcast_multiply_fusion.6), kind=kOutput, calls=%fused_computation.8.clone.1 | convolution fusion | flops 273678336 | bytes 9438208 | tf_op jit(solution)/shard_map/while/body/eval_jaxpr/vmap(pad,pbd->ab)/dot_general | solution.py:21
  439.1 153.2 %all-reduce.3.cloned.1.call-done = f32[192,2,4096]{2,1,0:T(2,128)} async-done(((f32[192,2,4096]{2,1,0:T(2,128)}), f32[192,2,4096]{2,1,0:T(2,128)}) %all-reduce.3.cloned.1.call-update) | async-done | bytes 6291472
  (198 shorter events, 215.2 us)
Async XLA Ops:
  7.2 431.6 %copy-start = (f32[48]{0:T(128)S(1)}, f32[48]{0:T(128)}, u32[]{:S(2)}) copy-start(f32[48]{0:T(128)} %param.15) | copy-start | bytes 580
  7.2 65.5 %all-gather.3.cloned.1.call-start = ((), (), s32[]{:S(2)}) async-start(), calls=%async_computation | async-start | bytes 3244032 | tf_op jit(solution)/shard_map/all_gather | solution.py:35
  7.9 584.3 %all-reduce.3.cloned.1.call-start = ((), (), s32[]{:S(2)}) async-start(), calls=%async_computation.1 | async-start | bytes 12582912
  437.4 0.7 copy-start.2
  437.4 0.9 copy-start.3
  437.5 154.8 %copy-start.1 = (bf16[6,2,4096]{2,1,0:T(2,128)(2,1)S(1)}, bf16[6,2,4096]{2,1,0:T(2,128)(2,1)}, u32[]{:S(2)}) copy-start(bf16[6,2,4096]{2,1,0:T(2,128)(2,1)} %param.11) | copy-start | bytes 294916
Sparse Core Ops, SparseCore 0:
  10.8 61.7 all-gather.2
  437.6 154.6 all-reduce.2
where the time goes:
time: 602 us; the launch traced here: 601 us
  local copies, waits for them, and re-layouts  216 us (36%)
  waiting for transfers between devices  173 us (29%)
  matrix products  145 us (24%)
  blocking collectives  43.6 us (7%)
  between operations  14.1 us (2%)
  other arithmetic  7.69 us (1%)
    gather x24, local copies, waits for them, and re-layouts, per_block(): picked = jnp.take(ints_ac, items[0], axis=0)  173 us
    unnamed x3, waiting for transfers between devices  154 us
    dot_general x12, matrix products, contract(): jnp.einsum('pad,pbd->ab', first, masked_b, preferred_element_type=jnp.flo...  72.4 us
    dot_general x12, matrix products, contract(): jnp.einsum('pad,pbd->ab', second, masked_b, preferred_element_type=jnp.fl...  72.3 us
    all_gather x1, blocking collectives, body(): lax.all_gather(mask_half, ('pair', 'aux'), axis=0, tiled=True)  43.6 us
    all_gather x1, waiting for transfers between devices, body(): lax.all_gather(amplitudes, ('pair', 'aux'), axis=0, tiled=True)  19.6 us
    dynamic_slice x24, local copies, waits for them, and re-layouts, body(): lax.map(per_block, (slot_pair.reshape(turns, batch), every_amps.reshape(t...  15.6 us
    dynamic_update_slice x12, local copies, waits for them, and re-layouts, body(): lax.map(per_block, (slot_pair.reshape(turns, batch), every_amps.reshape(t...  14.6 us
  transfers between devices with their start and end apart: 2, of which 2 were waited for; matrix products, arithmetic and copies ran while one was open for 0% of the time, Pallas kernels for 0%

commit v1 on v0

v1 whole, which is shorter than its diff:
```python
import jax
import jax.numpy as jnp
from jax import lax
from jax.experimental import pallas as pl
from jax.experimental.pallas import tpu as pltpu
from jax.sharding import PartitionSpec as P

GROUP = 8


def exchange_kernel(group, width, order_ref, *refs):
    blocks, amps_ref, out_ref, rows_ref = refs[:group], refs[group], refs[group + 1], refs[group + 2]
    lanes = 2 * width
    aux = blocks[0].shape[1]
    chunks = width * width // lanes
    half_t = lax.broadcasted_iota(jnp.int32, (width, lanes), 1) < width
    half_b = lax.broadcasted_iota(jnp.int32, (chunks, lanes), 1) < width
    for slot in range(group):
        block = blocks[slot]
        for chunk in range(chunks):
            rows_ref[slot, pl.ds(chunk * aux, aux), :] = block[
                0, :, pl.ds(chunk * lanes, lanes)
            ].astype(jnp.float32)
        pieces = []
        for pair in range(aux // 2):
            first = rows_ref[slot, pl.ds(2 * pair, chunks, stride=aux), :]
            second = rows_ref[slot, pl.ds(2 * pair + 1, chunks, stride=aux), :]
            even = jnp.where(half_b, first, pltpu.roll(second, width, 1))
            odd = jnp.where(half_b, pltpu.roll(first, width, 1), second)
            pieces.append(jnp.concatenate([even, odd], axis=0).astype(jnp.bfloat16))
        stacked = jnp.concatenate(pieces, axis=0)
        amps = amps_ref[slot].astype(jnp.float32)
        turned = pltpu.roll(amps, width, 1)
        none = jnp.zeros_like(amps)
        weights = jnp.concatenate(
            [
                jnp.concatenate([jnp.where(half_t, amps, none), jnp.where(half_t, none, turned)], axis=0),
                jnp.concatenate([jnp.where(half_t, turned, none), jnp.where(half_t, none, amps)], axis=0),
            ],
            axis=1,
        ).astype(jnp.bfloat16)
        inner = jnp.dot(stacked, weights, preferred_element_type=jnp.float32).astype(jnp.bfloat16)
        left = jnp.concatenate(pieces, axis=1)
        right = jnp.concatenate(
            [
                jnp.concatenate(
                    [
                        inner[pair * width : (pair + 1) * width, k * lanes : (k + 1) * lanes]
                        for pair in range(aux // 2)
                    ],
                    axis=1,
                )
                for k in range(2)
            ],
            axis=0,
        )
        out_ref[slot] = lax.dot_general(
            left, right, (((1,), (1,)), ((), ())), preferred_element_type=jnp.float32
        ).astype(out_ref.dtype)


def partials(ints_ac, slot_pair, amps):
    count, width, lanes = amps.shape
    aux = ints_ac.shape[1]
    group = max(g for g in range(1, GROUP + 1) if count % g == 0)

    def block_map(offset):
        return lambda step, order: (order[step * group + offset], 0, 0)

    return pl.pallas_call(
        lambda *refs: exchange_kernel(group, width, *refs),
        grid_spec=pltpu.PrefetchScalarGridSpec(
            num_scalar_prefetch=1,
            grid=(count // group,),
            in_specs=[
                pl.BlockSpec((1, aux, width * width), block_map(offset)) for offset in range(group)
            ]
            + [pl.BlockSpec((group, width, lanes), lambda step, order: (step, 0, 0))],
            out_specs=pl.BlockSpec((group, width, lanes), lambda step, order: (step, 0, 0)),
            scratch_shapes=[pltpu.VMEM((group, aux * width // 2, lanes), jnp.float32)],
        ),
        out_shape=jax.ShapeDtypeStruct((count, width, lanes), jnp.bfloat16),
        cost_estimate=pl.CostEstimate(
            flops=8 * count * aux * width**3,
            bytes_accessed=ints_ac.size * 2 + amps.size * 4,
            transcendentals=0,
        ),
        name="exchange",
    )(slot_pair, *([ints_ac] * group), amps)


def body(ints_ac, slot_pair, amplitudes, ranks, pair_occ, pno_energy, occ_energy):
    width = pno_energy.shape[1]
    local = amplitudes.shape[0]
    positions = jnp.arange(width, dtype=jnp.int32)
    masks = (positions[None, :] < ranks[:, None]).astype(jnp.float32)
    square = masks[:, :, None] * masks[:, None, :]
    masked_t = amplitudes.astype(jnp.float32).reshape(local, 2, width, width) * square[:, None]
    own = masked_t.astype(jnp.bfloat16).transpose(0, 2, 1, 3).reshape(local, width, 2 * width)
    every = lax.all_gather(own, ("pair", "aux"), axis=0, tiled=True)
    out = partials(ints_ac, slot_pair, every)
    parts = lax.all_to_all(out, ("pair", "aux"), 0, 0, tiled=True)
    parts = parts.reshape(-1, local, width, 2 * width)
    summed = parts.astype(jnp.float32).sum(axis=0)
    source = (positions % 2) * (width // 2) + positions // 2
    place = (positions[:, None] == source[None, :]).astype(jnp.float32)
    split = summed.reshape(local, width, 2, width)
    residual = jnp.einsum(
        "jykx,xa,yb->jkab", split, place, place, precision=lax.Precision.HIGHEST
    )
    residual = residual * square[:, None]
    onehot = (
        pair_occ[:, :, None] == jnp.arange(occ_energy.shape[0], dtype=jnp.int32)[None, None, :]
    ).astype(jnp.float32)
    occ_pair = jnp.einsum("jko,o->jk", onehot, occ_energy, precision=lax.Precision.HIGHEST)
    denom = (
        pno_energy[:, :, None]
        + pno_energy[:, None, :]
        - (occ_pair[:, 0] + occ_pair[:, 1])[:, None, None]
    )
    updated = (masked_t - residual / denom[:, None]) * square[:, None]
    return (
        residual.reshape(local, 2, width * width),
        updated.reshape(local, 2, width * width).astype(jnp.bfloat16),
    )


def solution(mesh):
    placed = (
        P(None, ("pair", "aux"), None),
        P(),
        P(("pair", "aux"), None, None),
        P(("pair", "aux")),
        P(("pair", "aux"), None),
        P(("pair", "aux"), None),
        P(),
    )
    return jax.shard_map(
        body,
        mesh=mesh,
        in_specs=placed,
        out_specs=(P(("pair", "aux"), None, None), P(("pair", "aux"), None, None)),
        check_vma=False,
    )
```

time: 602 us -> 211 us (0.35)
  local copies, waits for them, and re-layouts: 216 us -> 6.38 us
  matrix products: 145 us -> 2.2 us
  Pallas kernels: 0 us -> 47.9 us
  blocking collectives: 43.6 us -> 0 us
  waiting for transfers between devices: 173 us -> 133 us
    gather x24 -> x0, local copies, waits for them, and re-layouts: 173 us -> none  [per_block(): picked = jnp.take(ints_ac, items[0], axis=0)]
    unnamed x3 -> x1, waiting for transfers between devices: 154 us -> 0.02 us
    dot_general x24 -> x2, matrix products: 145 us -> 2.08 us  [body(): jnp.einsum('jykx,xa,yb->jkab', split, place, place, precision=lax.Precisi...]
    all_to_all x0 -> x1, waiting for transfers between devices: none -> 71.3 us  [body(): parts = lax.all_to_all(out, ('pair', 'aux'), 0, 0, tiled=True)]
    pallas_call x0 -> x1, Pallas kernels: none -> 47.9 us  [partials(): pl.pallas_call(lambda *refs: exchange_kernel(group, width, *refs), grid_s...]
    all_gather x1 -> x0, blocking collectives: 43.6 us -> none  [body(): lax.all_gather(mask_half, ('pair', 'aux'), axis=0, tiled=True)]
    all_gather x1, waiting for transfers between devices: 19.6 us -> 62 us  [body(): every = lax.all_gather(own, ('pair', 'aux'), axis=0, tiled=True)]
    dynamic_slice x24 -> x0, local copies, waits for them, and re-layouts: 15.6 us -> none  [body(): lax.map(per_block, (slot_pair.reshape(turns, batch), every_amps.reshape(t...]
where the time goes in v1:
time: 211 us
  waiting for transfers between devices  133 us (63%)
  Pallas kernels  47.9 us (23%)
  between operations  14.1 us (7%)
  local copies, waits for them, and re-layouts  6.38 us (3%)
  other arithmetic  3.82 us (2%)
  starting transfers between devices  3.37 us (2%)
  matrix products  2.2 us (1%)
    all_to_all x1, waiting for transfers between devices, body(): parts = lax.all_to_all(out, ('pair', 'aux'), 0, 0, tiled=True)  71.3 us
    all_gather x1, waiting for transfers between devices, body(): every = lax.all_gather(own, ('pair', 'aux'), axis=0, tiled=True)  62 us
    pallas_call x1, Pallas kernels, partials(): pl.pallas_call(lambda *refs: exchange_kernel(group, width, *refs), grid_s...  47.9 us
  transfers between devices with their start and end apart: 2, of which 2 were waited for; matrix products, arithmetic and copies ran while one was open for 0% of the time, Pallas kernels for 0%

profile of v1, /device:TPU:0, one launch (start us, length us, event | category | flops | bytes accessed | tf_op | source)
XLA Modules:
  0.0 211.1 jit_solution(4877332694024305031)
XLA Ops:
  7.2 0.0 copy-start
  7.2 0.0 all-gather.2.cloned.1.call-start
  7.2 1.0 reshape.106
  8.3 0.8 copy.18
  9.0 0.1 iota_compare_fusion.1
  9.1 0.0 copy-done
  9.1 0.1 fusion.10
  9.3 0.8 fusion.12
  10.1 1.6 add_subtract_fusion
  11.6 0.0 copy-start.1
  11.6 0.7 copy-done.1
  12.4 0.2 copy.15
  12.6 0.8 reshape.102
  13.4 0.0 all-gather.2.cloned.1.call-update
  13.4 62.0 %all-gather.2.cloned.1.call-done.refs_9_ = bf16[192,64,128]{2,1,0:T(8,128)(2,1)} async-done(((bf16[6,64,128]{2,1,0:T(8,128)(2,1)}), bf16[192,64,128]{2,1,0:T(8,128)(2,1)}) %all-gather.2.cloned.1.call-update) | async-done | bytes 3145744 | tf_op jit(solution)/shard_map/all_gather | solution.py:100
  75.4 47.9 %exchange.1 = bf16[192,64,128]{2,1,0:T(8,128)(2,1)} custom-call(s32[192]{0:T(256)} %refs_0_.1, bf16[192,16,4096]{2,1,0:T(8,128)(2,1)} %refs_8_.1, bf16[192,16,4096]{2,1,0:T(8,128)(2,1)} %refs_8_.1, bf16[192,16,4096]{2,1,0:T(8,128)(2,1)} %refs_8_.1, bf16[192,16,4096]{2,1,0:T(8,128)(2,1)} %refs_8_.1, bf16[192,16,4096]{2,1,0:T(8,128)(2,1)} %refs_8_.1, ...), custom_call_target="tpu_custom_call" | custom-call | flops 6442450944 | bytes 31457280 | tf_op jit(solution)/shard_map/exchange/pallas_call | solution.py:70
  123.3 3.3 %all-to-all-start = ((bf16[192,64,128]{2,1,0:T(8,128)(2,1)}), bf16[192,64,128]{2,1,0:T(8,128)(2,1)S(1)}, u32[]{:S(2)}, u32[]{:S(2)}) async-start(bf16[192,64,128]{2,1,0:T(8,128)(2,1)} %exchange.1), calls=%async_computation | async-start | bytes 6291456 | tf_op jit(solution)/shard_map/all_to_all | solution.py:102
  126.6 71.3 %all-to-all-done = bf16[192,64,128]{2,1,0:T(8,128)(2,1)S(1)} async-done(((bf16[192,64,128]{2,1,0:T(8,128)(2,1)}), bf16[192,64,128]{2,1,0:T(8,128)(2,1)S(1)}, u32[]{:S(2)}, u32[]{:S(2)}) %all-to-all-start) | async-done | bytes 3145760 | tf_op jit(solution)/shard_map/all_to_all | solution.py:102
  197.9 1.3 convert_reduce_fusion
  199.2 1.2 reshape.103
  200.4 0.7 fusion.1
  201.1 1.4 multiply_convert_fusion
  202.5 0.9 reshape.104
  203.4 0.8 convert_element_type.34
  (3 shorter events, 0.1 us)
Async XLA Ops:
  7.2 2.0 copy-start
  7.2 68.2 %all-gather.2.cloned.1.call-start = ((), (), s32[]{:S(2)}) async-start(), calls=%async_computation.1 | async-start | bytes 3244032 | tf_op jit(solution)/shard_map/all_gather | solution.py:100
  11.6 0.7 copy-start.1
  123.3 74.7 %all-to-all-start = ((bf16[192,64,128]{2,1,0:T(8,128)(2,1)}), bf16[192,64,128]{2,1,0:T(8,128)(2,1)S(1)}, u32[]{:S(2)}, u32[]{:S(2)}) async-start(bf16[192,64,128]{2,1,0:T(8,128)(2,1)} %exchange.1), calls=%async_computation | async-start | bytes 6291456 | tf_op jit(solution)/shard_map/all_to_all | solution.py:102
Sparse Core Ops, SparseCore 0:
  13.5 61.7 all-gather.1
